TPU v7x, 32 devices: a whole 2x2x4 slice. The times are simulated.
32 devices in a mesh: gx: 2 (over x), gy: 4 (over z), gz: 4 (over y, core).
Axes of the slice: x: 2, y: 2, z: 4, core: 2. Of those that a mesh axis runs over, the one named last changes fastest.
Arguments:
- pair_map: bfloat16 [160, 160, 128], P('gx', ('gy', 'gz')), may hold values from -6 to 6
- residue_mask: int32 [160], replicated, may hold values 0 or 1
- proj_weight: bfloat16 [128, 512], replicated, may hold values from -0.5 to 0.5
- gate_weight: bfloat16 [128, 128], replicated, may hold values from -0.5 to 0.5
- out_weight: bfloat16 [128, 128], replicated, may hold values from -0.5 to 0.5
Outputs:
- update: bfloat16 [160, 160, 128], P('gx', ('gy', 'gz'))
All inputs are finite; a program needn't handle non-finite values.
Results may differ from a plain program's by a relative error of at most 0.009.
Values may be sent and summed in bfloat16 or wider, within the bound.
A program may use at most 128 MiB of HBM per device.

v0:
```python
import functools

import jax
import jax.numpy as jnp
from jax import lax
from jax.experimental import pallas as pl
from jax.experimental.pallas import tpu as pltpu
from jax.sharding import PartitionSpec as P

epsilon = 1.0


def partner_2(x, axis, bit):
    return lax.ppermute(x, axis, [(i, i ^ 1 << bit) for i in range(lax.axis_size(axis))])


def layer_norm_lead(values):
    average = jnp.mean(values, axis=0, keepdims=True)
    centred = values - average
    variance = jnp.mean(centred * centred, axis=0, keepdims=True)
    return centred * lax.rsqrt(variance + epsilon)


def layer_norm_last(values):
    average = jnp.mean(values, axis=-1, keepdims=True)
    centred = values - average
    variance = jnp.mean(centred * centred, axis=-1, keepdims=True)
    return centred * lax.rsqrt(variance + epsilon)


def swap_with(values, bit):
    return partner_2(values, "gx", bit)


def pair_join(values, bit, position):
    partner = swap_with(values, bit)
    mine_first = position // 2**bit % 2 == 0
    return jnp.where(
        mine_first,
        jnp.concatenate([values, partner], axis=1),
        jnp.concatenate([partner, values], axis=1),
    )


def whole_channels(gathered, out_weight, gate_value):
    hidden, row_count, col_count = gathered.shape
    normed_tri = layer_norm_lead(gathered.astype(jnp.float32)).astype(jnp.bfloat16)
    mixed_out = lax.dot_general(
        normed_tri.reshape(hidden, row_count * col_count),
        out_weight,
        (((0,), (0,)), ((), ())),
        preferred_element_type=jnp.float32,
    )
    return gate_value * mixed_out.reshape(row_count, col_count, out_weight.shape[1])


def local(pair_map, residue_mask, proj_weight, gate_weight, out_weight):
    row_count, col_count, chan_count = pair_map.shape
    hidden = out_weight.shape[0]
    residues = residue_mask.shape[0]
    along_x = lax.axis_size("gx")
    along_y = lax.axis_size("gy")
    along_z = lax.axis_size("gz")
    mask_float = residue_mask.astype(jnp.float32)
    row_mask = lax.dynamic_slice_in_dim(mask_float, lax.axis_index("gx") * row_count, row_count)
    col_mask = lax.dynamic_slice_in_dim(
        mask_float, (lax.axis_index("gy") * along_z + lax.axis_index("gz")) * col_count, col_count
    )
    normed = layer_norm_last(pair_map.astype(jnp.float32)).astype(jnp.bfloat16)
    flattened = normed.reshape(row_count * col_count, chan_count)
    projected = lax.dot_general(
        proj_weight, flattened, (((0,), (1,)), ((), ())), preferred_element_type=jnp.float32
    ).reshape(4 * hidden, row_count, col_count)
    pair_mask = (row_mask[:, None] * col_mask[None, :])[None, :, :]
    left_proj = (
        jax.nn.sigmoid(projected[:hidden]) * projected[hidden : 2 * hidden] * pair_mask
    ).astype(jnp.bfloat16)
    right_proj = (
        jax.nn.sigmoid(projected[2 * hidden : 3 * hidden]) * projected[3 * hidden :] * pair_mask
    ).astype(jnp.bfloat16)
    gate_value = jax.nn.sigmoid(
        jnp.dot(flattened, gate_weight, preferred_element_type=jnp.float32)
    ).reshape(row_count, col_count, chan_count)
    group_count = along_y * along_z
    group_chan = hidden // group_count
    left_group, right_group = (
        lax.all_to_all(left_proj, ("gy", "gz"), split_axis=0, concat_axis=2, tiled=True),
        lax.all_to_all(right_proj, ("gy", "gz"), split_axis=0, concat_axis=2, tiled=True),
    )
    levels = along_x.bit_length() - 1
    low_bits = levels // 2
    high_count = 2 ** (levels - low_bits)
    low_count = 2**low_bits
    position = lax.axis_index("gx")
    left_tile = left_group
    for bit in range(low_bits):
        left_tile = pair_join(left_tile, bit, position)
    right_tile = right_group
    for bit in range(low_bits, levels):
        right_tile = pair_join(right_tile, bit, position)
    block_tile = jnp.einsum(
        "cik,cjk->cij", left_tile, right_tile, preferred_element_type=jnp.float32
    ).astype(jnp.bfloat16)
    for bit in range(low_bits):
        current = block_tile.shape[1]
        span = block_tile.shape[2]
        shaped = block_tile.reshape(group_chan, current // (2 * row_count), 2, row_count, span)
        own_bit = position // 2**bit % 2
        kept = lax.dynamic_index_in_dim(shaped, own_bit, axis=2, keepdims=False).reshape(
            group_chan, current // 2, span
        )
        sent = lax.dynamic_index_in_dim(shaped, 1 - own_bit, axis=2, keepdims=False).reshape(
            group_chan, current // 2, span
        )
        arrived = swap_with(sent, bit)
        block_tile = jnp.where(
            own_bit == 0,
            jnp.concatenate([kept, arrived], axis=2),
            jnp.concatenate([arrived, kept], axis=2),
        )
    block_tile = (
        block_tile.reshape(group_chan, row_count, low_count, high_count, row_count)
        .transpose(0, 1, 3, 2, 4)
        .reshape(group_chan, row_count, residues)
    )
    gathered = lax.all_to_all(block_tile, ("gy", "gz"), split_axis=2, concat_axis=0, tiled=True)
    update = whole_channels(gathered, out_weight, gate_value)
    return update.astype(jnp.bfloat16)


MESH = pl.DeviceIdType.MESH
LANES = 128
PIECES = 1
VMEM_GRANT = 67043328
VMEM_BUDGET = 48 * 2**20


def up(value, step):
    return -(-value // step) * step


def fused_kernel(
    along_y, along_z,
    pair_hbm, mask_hbm, proj_hbm, gate_hbm, out_w_hbm, out_ref,
    pair_ref, mask_ref, proj_ref, gate_ref, out_w_ref,
    normed_bf, masked_bf, gate_f32, send_r, recv_r, recv_x, send_l, recv_l,
    left_s, right_s, tri_s, send_b, recv_b,
    ssem_r, rsem_r, ssem_x, rsem_x, ssem_l, rsem_l, ssem_b, rsem_b, own_sem, load_sem,
):
    cols, rows, chans = pair_ref.shape
    hidden = out_w_ref.shape[0]
    groups = along_y * along_z
    gc = hidden // groups
    hc = gc // PIECES
    flat = rows * cols
    residues = mask_ref.shape[1]
    px, py, pz = lax.axis_index("gx"), lax.axis_index("gy"), lax.axis_index("gz")
    me = py * along_z + pz

    def place(d):
        return (px, d // along_z, d % along_z)

    partner = (1 - px, py, pz)
    barrier = pltpu.get_barrier_semaphore()

    def greet(o, carry):
        pl.semaphore_signal(barrier, inc=1, device_id=place((me + o) % groups), device_id_type=MESH)
        return carry

    lax.fori_loop(1, groups, greet, 0)
    pl.semaphore_signal(barrier, inc=1, device_id=partner, device_id_type=MESH)

    loads = [
        pltpu.make_async_copy(source, target, load_sem.at[n])
        for n, (source, target) in enumerate(
            (
                (pair_hbm, pair_ref), (mask_hbm, mask_ref), (proj_hbm, proj_ref),
                (gate_hbm, gate_ref), (out_w_hbm, out_w_ref),
            )
        )
    ]
    for load in loads:
        load.start()
    loads[0].wait()
    loads[1].wait()

    mask_f = mask_ref[...].astype(jnp.float32)
    lane = lax.broadcasted_iota(jnp.int32, (rows, residues), 1)
    sub = lax.broadcasted_iota(jnp.int32, (rows, residues), 0)
    row_mask = jnp.sum(jnp.where(lane == sub + px * rows, mask_f, 0.0), axis=1, keepdims=True)
    lane_row = lax.broadcasted_iota(jnp.int32, (1, residues), 1)
    for k in range(cols):
        col_mask = jnp.sum(
            jnp.where(lane_row == me * cols + k, mask_f, 0.0), axis=1, keepdims=True
        )
        normed = layer_norm_last(pair_ref[k].astype(jnp.float32)).astype(jnp.bfloat16)
        normed_bf[k * rows : (k + 1) * rows, :] = normed
        masked_bf[k * rows : (k + 1) * rows, :] = (
            normed.astype(jnp.float32) * (row_mask * col_mask)
        ).astype(jnp.bfloat16)

    loads[2].wait()
    proj_t = proj_ref[...].astype(jnp.float32).T.astype(jnp.bfloat16)
    masked = masked_bf[...]

    def project(first, count):
        return lax.dot_general(
            proj_t[first : first + count], masked, (((1,), (1,)), ((), ())),
            preferred_element_type=jnp.float32,
        )

    def copy_r(d, slot):
        return pltpu.make_async_remote_copy(
            src_ref=send_r.at[d], dst_ref=recv_r.at[slot], send_sem=ssem_r.at[d],
            recv_sem=rsem_r.at[slot], device_id=place(d), device_id_type=MESH,
        )

    def copy_l(h, d, slot):
        return pltpu.make_async_remote_copy(
            src_ref=send_l.at[h, d], dst_ref=recv_l.at[h, slot], send_sem=ssem_l.at[h, d],
            recv_sem=rsem_l.at[h, slot], device_id=place(d), device_id_type=MESH,
        )

    def copy_x(s):
        return pltpu.make_async_remote_copy(
            src_ref=recv_r.at[s], dst_ref=recv_x.at[s], send_sem=ssem_x.at[s],
            recv_sem=rsem_x.at[s], device_id=partner, device_id_type=MESH,
        )

    def copy_b(h, d, slot):
        return pltpu.make_async_remote_copy(
            src_ref=send_b.at[h, d], dst_ref=recv_b.at[h, slot], send_sem=ssem_b.at[h, d],
            recv_sem=rsem_b.at[h, slot], device_id=place(d), device_id_type=MESH,
        )

    step = 4 * gc

    def gated(first, side):
        base = 2 * side * hidden + first
        return jax.nn.sigmoid(project(base, step)) * project(base + hidden, step)

    for first in range(0, hidden, step):
        value = gated(first, 1)
        for part in range(step // gc):
            send_r[first // gc + part, :, 0:flat] = value[
                part * gc : (part + 1) * gc
            ].astype(jnp.bfloat16)

    pl.semaphore_wait(barrier, groups)

    def start_r(o, carry):
        copy_r((me + o) % groups, me).start()
        return carry

    lax.fori_loop(1, groups, start_r, 0)
    own_r = pltpu.make_async_copy(send_r.at[me], recv_r.at[me], own_sem.at[0])
    own_r.start()

    for first in range(0, hidden, step):
        value = gated(first, 0)
        for part in range(step // gc):
            for h in range(PIECES):
                low = part * gc + h * hc
                send_l[h, first // gc + part, :, 0:flat] = value[low : low + hc].astype(jnp.bfloat16)

    for h in range(PIECES):

        def start_l(o, carry, h=h):
            copy_l(h, (me + o) % groups, me).start()
            return carry

        lax.fori_loop(1, groups, start_l, 0)

    loads[3].wait()
    loads[4].wait()
    gate_f32[...] = jax.nn.sigmoid(
        jnp.dot(normed_bf[...], gate_ref[...], preferred_element_type=jnp.float32)
    )

    def spread(value, target, s, first, count):
        value = value.astype(jnp.float32)
        for k in range(cols):
            at = pl.multiple_of((s * cols + k) * gc, gc)
            target[pl.ds(at + first, count), 0:rows] = value[:, k * rows : (k + 1) * rows]

    own_r.wait()

    def take_r(o, carry):
        s = (me + groups - o) % groups

        @pl.when(o > 0)
        def _():
            copy_r(s, s).wait_recv()

        copy_x(s).start()
        spread(recv_r[s], right_s.at[px], s, 0, gc)
        return carry

    lax.fori_loop(0, groups, take_r, 0)

    def take_x(o, carry):
        s = (me + groups - o) % groups
        copy_x(s).wait_recv()
        spread(recv_x[s], right_s.at[1 - px], s, 0, gc)
        return carry

    lax.fori_loop(0, groups, take_x, 0)

    for h in range(PIECES):
        spread(send_l[h, me], left_s, me, h * hc, hc)

        def take_l(o, carry, h=h):
            s = (me + groups - o) % groups
            copy_l(h, s, s).wait_recv()
            spread(recv_l[h, s], left_s, s, h * hc, hc)
            return carry

        lax.fori_loop(1, groups, take_l, 0)

        for c in range(h * hc, (h + 1) * hc):
            left = left_s[pl.ds(c, residues, stride=gc), :].astype(jnp.bfloat16)
            for half in range(2):
                right = right_s[half, pl.ds(c, residues, stride=gc), :].astype(jnp.bfloat16)
                block = lax.dot_general(
                    right, left, (((0,), (0,)), ((), ())), preferred_element_type=jnp.float32
                )
                tri_s[pl.ds(half * rows * gc + c, rows, stride=gc), :] = block[0:rows]

        def pack_b(d, h=h):
            pieces = []
            for j in range(cols):
                at = pl.multiple_of((d * cols + j) * gc, gc)
                pieces.append(tri_s[pl.ds(at + h * hc, hc), 0:rows])
            return jnp.concatenate(pieces, axis=1).astype(jnp.bfloat16)

        def start_b(o, carry, h=h):
            d = (me + o) % groups
            send_b[h, d, :, 0:flat] = pack_b(d)
            copy_b(h, d, me).start()
            return carry

        lax.fori_loop(1, groups, start_b, 0)
        recv_b[h, me, :, 0:flat] = pack_b(me)

    for h in range(PIECES):

        def take_b(o, carry, h=h):
            s = (me + groups - o) % groups
            copy_b(h, s, s).wait_recv()
            return carry

        lax.fori_loop(1, groups, take_b, 0)

    triangle = jnp.concatenate(
        [recv_b[h, :, :, 0:flat].astype(jnp.float32) for h in range(PIECES)], axis=1
    ).reshape(hidden, flat)
    normed_tri = layer_norm_lead(triangle).astype(jnp.bfloat16)
    mixed = lax.dot_general(
        normed_tri, out_w_ref[...], (((0,), (0,)), ((), ())), preferred_element_type=jnp.float32
    )
    update = gate_f32[...] * mixed
    for j in range(cols):
        out_ref[j] = update[j * rows : (j + 1) * rows].astype(jnp.bfloat16)

    def finish(o, carry):
        d = (me + o) % groups
        copy_r(d, me).wait_send()
        for h in range(PIECES):
            copy_l(h, d, me).wait_send()
            copy_b(h, d, me).wait_send()
        return carry

    lax.fori_loop(1, groups, finish, 0)

    def finish_x(s, carry):
        copy_x(s).wait_send()
        return carry

    lax.fori_loop(0, groups, finish_x, 0)


def scratch_list(rows, cols, chans, hidden, groups, residues):
    gc = hidden // groups
    flat = up(rows * cols, LANES)
    hc = gc // PIECES
    bf, f32 = jnp.bfloat16, jnp.float32
    return [
        ((cols, rows, chans), bf),
        ((1, residues), jnp.int32),
        ((chans, 4 * hidden), bf),
        ((chans, chans), bf),
        ((hidden, chans), bf),
        ((rows * cols, chans), bf),
        ((rows * cols, chans), bf),
        ((rows * cols, chans), f32),
        ((groups, gc, flat), bf),
        ((groups, gc, flat), bf),
        ((groups, gc, flat), bf),
        ((PIECES, groups, hc, flat), bf),
        ((PIECES, groups, hc, flat), bf),
        ((residues * gc, LANES), f32),
        ((2, residues * gc, LANES), f32),
        ((residues * gc, LANES), f32),
        ((PIECES, groups, hc, flat), bf),
        ((PIECES, groups, hc, flat), bf),
    ]


def fits_kernel(sizes, rows, cols, chans, hidden, residues):
    groups = sizes["gy"] * sizes["gz"]
    if sizes["gx"] != 2 or hidden % (4 * groups) or hidden // groups != 8:
        return False
    if chans != LANES or rows > LANES or rows % 16:
        return False
    total = 0
    for shape, kind in scratch_list(rows, cols, chans, hidden, groups, residues):
        count = 1
        for extent in shape:
            count *= extent
        total += count * jnp.dtype(kind).itemsize
    return total < VMEM_BUDGET // 4


def local_fused(sizes, pair_map, residue_mask, proj_weight, gate_weight, out_weight):
    rows, cols, chans = pair_map.shape
    hidden = out_weight.shape[0]
    residues = residue_mask.shape[0]
    if not fits_kernel(sizes, rows, cols, chans, hidden, residues):
        return local(pair_map, residue_mask, proj_weight, gate_weight, out_weight)
    groups = sizes["gy"] * sizes["gz"]
    dma = pltpu.SemaphoreType.DMA((groups,))
    dma_halves = pltpu.SemaphoreType.DMA((PIECES, groups))
    vmem = pl.BlockSpec(memory_space=pltpu.VMEM)
    turned = pl.pallas_call(
        functools.partial(fused_kernel, sizes["gy"], sizes["gz"]),
        out_shape=jax.ShapeDtypeStruct((cols, rows, chans), jnp.bfloat16),
        in_specs=[pl.BlockSpec(memory_space=pltpu.HBM)] * 5,
        out_specs=vmem,
        scratch_shapes=[
            pltpu.VMEM(shape, kind)
            for shape, kind in scratch_list(rows, cols, chans, hidden, groups, residues)
        ]
        + [dma] * 4
        + [dma_halves] * 4
        + [pltpu.SemaphoreType.DMA((1,)), pltpu.SemaphoreType.DMA((5,))],
        compiler_params=pltpu.CompilerParams(
            collective_id=0, has_side_effects=True, vmem_limit_bytes=VMEM_GRANT
        ),
    )(
        pair_map.transpose(1, 0, 2), residue_mask.reshape(1, residues),
        proj_weight, gate_weight, out_weight,
    )
    return turned.transpose(1, 0, 2)


def solution(mesh):
    placed = (P("gx", ("gy", "gz"), None), P(), P(), P(), P())
    return jax.shard_map(
        functools.partial(local_fused, dict(mesh.shape)), mesh=mesh, in_specs=placed, out_specs=P("gx", ("gy", "gz"), None), check_vma=False
    )
```

profile of v0, /device:TPU:0, one launch (start us, length us, event | category | flops | bytes accessed | tf_op | source)
XLA Modules:
  0.0 29.3 jit_solution(10142544383507697276)
XLA Ops:
  0.0 27.6 %shard_map.55 = bf16[10,80,128]{2,1,0:T(8,128)(2,1)} custom-call(bf16[10,80,128]{2,1,0:T(8,128)(2,1)} %bitcast.4, s32[1,160]{1,0:T(1,128)} %bitcast.5, bf16[128,512]{1,0:T(8,128)(2,1)} %proj_hbm.1, bf16[128,128]{1,0:T(8,128)(2,1)} %gate_hbm.1, bf16[128,128]{1,0:T(8,128)(2,1)} %out_w_hbm.1), custom_call_target="tpu_custom_call" | custom-call | tf_op jit(solution)/shard_map/pallas_call | solution.py:434
  27.6 1.6 %copy.7 = bf16[80,10,128]{2,0,1:T(8,128)(2,1)} copy(bf16[80,10,128]{2,0,1:T(8,128)(2,1)} %bitcast.3) | data formatting | bytes 409600
where the time goes:
time: 29.4 us; the launch traced here: 29.3 us
  Pallas kernels  27.6 us (94%)
  local copies, waits for them, and re-layouts  1.62 us (6%)
    pallas_call x1, Pallas kernels, local_fused(): pl.pallas_call(functools.partial(fused_kernel, sizes['gy'], sizes['gz']),...  27.6 us
    unnamed x1, local copies, waits for them, and re-layouts  1.62 us

commit v1 on v0

v1 whole, which is shorter than its diff:
```python
import functools

import jax
import jax.numpy as jnp
from jax import lax
from jax.experimental import pallas as pl
from jax.experimental.pallas import tpu as pltpu
from jax.sharding import PartitionSpec as P

epsilon = 1.0


def partner_2(x, axis, bit):
    return lax.ppermute(x, axis, [(i, i ^ 1 << bit) for i in range(lax.axis_size(axis))])


def layer_norm_lead(values):
    average = jnp.mean(values, axis=0, keepdims=True)
    centred = values - average
    variance = jnp.mean(centred * centred, axis=0, keepdims=True)
    return centred * lax.rsqrt(variance + epsilon)


def layer_norm_last(values):
    average = jnp.mean(values, axis=-1, keepdims=True)
    centred = values - average
    variance = jnp.mean(centred * centred, axis=-1, keepdims=True)
    return centred * lax.rsqrt(variance + epsilon)


def swap_with(values, bit):
    return partner_2(values, "gx", bit)


def pair_join(values, bit, position):
    partner = swap_with(values, bit)
    mine_first = position // 2**bit % 2 == 0
    return jnp.where(
        mine_first,
        jnp.concatenate([values, partner], axis=1),
        jnp.concatenate([partner, values], axis=1),
    )


def whole_channels(gathered, out_weight, gate_value):
    hidden, row_count, col_count = gathered.shape
    normed_tri = layer_norm_lead(gathered.astype(jnp.float32)).astype(jnp.bfloat16)
    mixed_out = lax.dot_general(
        normed_tri.reshape(hidden, row_count * col_count),
        out_weight,
        (((0,), (0,)), ((), ())),
        preferred_element_type=jnp.float32,
    )
    return gate_value * mixed_out.reshape(row_count, col_count, out_weight.shape[1])


def local(pair_map, residue_mask, proj_weight, gate_weight, out_weight):
    row_count, col_count, chan_count = pair_map.shape
    hidden = out_weight.shape[0]
    residues = residue_mask.shape[0]
    along_x = lax.axis_size("gx")
    along_y = lax.axis_size("gy")
    along_z = lax.axis_size("gz")
    mask_float = residue_mask.astype(jnp.float32)
    row_mask = lax.dynamic_slice_in_dim(mask_float, lax.axis_index("gx") * row_count, row_count)
    col_mask = lax.dynamic_slice_in_dim(
        mask_float, (lax.axis_index("gy") * along_z + lax.axis_index("gz")) * col_count, col_count
    )
    normed = layer_norm_last(pair_map.astype(jnp.float32)).astype(jnp.bfloat16)
    flattened = normed.reshape(row_count * col_count, chan_count)
    projected = lax.dot_general(
        proj_weight, flattened, (((0,), (1,)), ((), ())), preferred_element_type=jnp.float32
    ).reshape(4 * hidden, row_count, col_count)
    pair_mask = (row_mask[:, None] * col_mask[None, :])[None, :, :]
    left_proj = (
        jax.nn.sigmoid(projected[:hidden]) * projected[hidden : 2 * hidden] * pair_mask
    ).astype(jnp.bfloat16)
    right_proj = (
        jax.nn.sigmoid(projected[2 * hidden : 3 * hidden]) * projected[3 * hidden :] * pair_mask
    ).astype(jnp.bfloat16)
    gate_value = jax.nn.sigmoid(
        jnp.dot(flattened, gate_weight, preferred_element_type=jnp.float32)
    ).reshape(row_count, col_count, chan_count)
    group_count = along_y * along_z
    group_chan = hidden // group_count
    left_group, right_group = (
        lax.all_to_all(left_proj, ("gy", "gz"), split_axis=0, concat_axis=2, tiled=True),
        lax.all_to_all(right_proj, ("gy", "gz"), split_axis=0, concat_axis=2, tiled=True),
    )
    levels = along_x.bit_length() - 1
    low_bits = levels // 2
    high_count = 2 ** (levels - low_bits)
    low_count = 2**low_bits
    position = lax.axis_index("gx")
    left_tile = left_group
    for bit in range(low_bits):
        left_tile = pair_join(left_tile, bit, position)
    right_tile = right_group
    for bit in range(low_bits, levels):
        right_tile = pair_join(right_tile, bit, position)
    block_tile = jnp.einsum(
        "cik,cjk->cij", left_tile, right_tile, preferred_element_type=jnp.float32
    ).astype(jnp.bfloat16)
    for bit in range(low_bits):
        current = block_tile.shape[1]
        span = block_tile.shape[2]
        shaped = block_tile.reshape(group_chan, current // (2 * row_count), 2, row_count, span)
        own_bit = position // 2**bit % 2
        kept = lax.dynamic_index_in_dim(shaped, own_bit, axis=2, keepdims=False).reshape(
            group_chan, current // 2, span
        )
        sent = lax.dynamic_index_in_dim(shaped, 1 - own_bit, axis=2, keepdims=False).reshape(
            group_chan, current // 2, span
        )
        arrived = swap_with(sent, bit)
        block_tile = jnp.where(
            own_bit == 0,
            jnp.concatenate([kept, arrived], axis=2),
            jnp.concatenate([arrived, kept], axis=2),
        )
    block_tile = (
        block_tile.reshape(group_chan, row_count, low_count, high_count, row_count)
        .transpose(0, 1, 3, 2, 4)
        .reshape(group_chan, row_count, residues)
    )
    gathered = lax.all_to_all(block_tile, ("gy", "gz"), split_axis=2, concat_axis=0, tiled=True)
    update = whole_channels(gathered, out_weight, gate_value)
    return update.astype(jnp.bfloat16)


MESH = pl.DeviceIdType.MESH
LANES = 128
HALF_LANES = 64
VMEM_ALL = 67043328
VMEM_BUDGET = 48 * 2**20


def up(value, step):
    return -(-value // step) * step


def gate_by(gate, value):
    return (0.5 * value) * (1.0 + jnp.tanh(0.5 * gate))


def fused_kernel(
    along_y, along_z, main,
    pair_hbm, mask_hbm, proj_hbm, gate_hbm, out_w_hbm, out_ref,
    pair_ref, mask_ref, proj_ref, gate_ref, out_w_ref,
    proj_s, normed_bf, masked_bf, gate_f32, send_r, recv_r, recv_x, send_l, recv_l,
    left_s, edge_s, right_s, right_bf, tri_s, send_e, recv_e, send_b, recv_b,
    load_sem, send_sem, rsem_r, rsem_x, rsem_l, rsem_b,
):
    cols, rows, chans = pair_ref.shape
    hidden = out_w_ref.shape[0]
    groups = along_y * along_z
    gc = hidden // groups
    edge = rows - main
    flat_m, flat_e = main * cols, edge * cols
    flat = flat_m + flat_e
    wide = up(flat, LANES)
    residues = mask_ref.shape[1]
    px, py, pz = lax.axis_index("gx"), lax.axis_index("gy"), lax.axis_index("gz")
    me = py * along_z + pz
    side = py // (along_y // 2)
    middle = along_y // 2

    def place(d):
        return (px, d // along_z, d % along_z)

    far_a, far_b = (1 - side) * middle, (1 - side) * middle + 1
    sibling = side * middle + (py + 1) % middle

    def to(plane, n):
        return plane * along_z + (pz + n) % along_z

    def source(plane, n):
        return plane * along_z + (pz + along_z - n) % along_z

    def turn_of(s):
        return (pz + along_z - s % along_z) % along_z

    partner = (1 - px, py, pz)
    barrier = pltpu.get_barrier_semaphore()

    def greet(o, carry):
        pl.semaphore_signal(barrier, inc=1, device_id=place((me + o) % groups), device_id_type=MESH)
        return carry

    with jax.named_scope("greet"):
        lax.fori_loop(1, groups, greet, 0)
        pl.semaphore_signal(barrier, inc=1, device_id=partner, device_id_type=MESH)

    loads = [
        pltpu.make_async_copy(source, target, load_sem.at[n])
        for n, (source, target) in enumerate(
            (
                (pair_hbm, pair_ref), (mask_hbm, mask_ref), (proj_hbm, proj_ref),
                (gate_hbm, gate_ref), (out_w_hbm, out_w_ref),
            )
        )
    ]
    for load in loads:
        load.start()
    with jax.named_scope("waitload"):
        loads[1].wait()
        loads[2].wait()
        proj_s[...] = proj_ref[...].astype(jnp.float32).T.astype(jnp.bfloat16)
        loads[0].wait()

    with jax.named_scope("norm"):
        mask_f = mask_ref[...].astype(jnp.float32)
        lane = lax.broadcasted_iota(jnp.int32, (rows, residues), 1)
        sub = lax.broadcasted_iota(jnp.int32, (rows, residues), 0)
        row_mask = jnp.sum(jnp.where(lane == sub + px * rows, mask_f, 0.0), axis=1, keepdims=True)
        lane_row = lax.broadcasted_iota(jnp.int32, (1, residues), 1)
        for k in range(cols):
            col_mask = jnp.sum(
                jnp.where(lane_row == me * cols + k, mask_f, 0.0), axis=1, keepdims=True
            )
            normed = layer_norm_last(pair_ref[k].astype(jnp.float32)).astype(jnp.bfloat16)
            masked = (normed.astype(jnp.float32) * (row_mask * col_mask)).astype(jnp.bfloat16)
            for target, value in ((normed_bf, normed), (masked_bf, masked)):
                target[k * main : (k + 1) * main, :] = value[0:main]
                target[flat_m + k * edge : flat_m + (k + 1) * edge, :] = value[main:rows]

    half = hidden // 2
    half_groups = groups // 2

    def gated(base, first, low, high):
        both = jnp.concatenate(
            [
                proj_s[pl.ds(pl.multiple_of(base + first, half), half), :],
                proj_s[pl.ds(pl.multiple_of(base + hidden + first, half), half), :],
            ],
            axis=0,
        )
        both = lax.dot_general(
            both, masked_bf[low:high, :], (((1,), (1,)), ((), ())),
            preferred_element_type=jnp.float32,
        )
        return gate_by(both[0:half], both[half:])

    def copy_r(d, slot):
        return pltpu.make_async_remote_copy(
            src_ref=send_r.at[d], dst_ref=recv_r.at[slot], send_sem=send_sem.at[0],
            recv_sem=rsem_r.at[slot], device_id=place(d), device_id_type=MESH,
        )

    def copy_x(s, count=1):
        return pltpu.make_async_remote_copy(
            src_ref=recv_r.at[pl.ds(s, count), :, 0:wide], dst_ref=recv_x.at[pl.ds(s, count)],
            send_sem=send_sem.at[1], recv_sem=rsem_x.at[turn_of(s)],
            device_id=partner, device_id_type=MESH,
        )

    def copy_many(source, target, kind, recv_sem, d, slot, count=1):
        return pltpu.make_async_remote_copy(
            src_ref=source.at[pl.ds(d, count)], dst_ref=target.at[pl.ds(slot, count)],
            send_sem=send_sem.at[kind], recv_sem=recv_sem, device_id=place(d),
            device_id_type=MESH,
        )

    def copy_l(d, slot, n, count=1):
        return copy_many(send_l, recv_l, 2, rsem_l.at[n], d, slot, count)

    def copy_e(d, slot, count=1):
        return copy_many(send_e, recv_e, 3, rsem_b.at[0], d, slot, count)

    def copy_b(d, slot, count=1):
        return copy_many(send_b, recv_b, 4, rsem_b.at[1], d, slot, count)

    for turn in range(2):
        first = (1 - side if turn == 0 else side) * half
        with jax.named_scope(f"gated_r{turn}"):
            value = gated(2 * hidden, first, 0, flat)
            extra = gated(0, first, flat_m, flat)
            value = jnp.concatenate([value, extra], axis=1)
            for part in range(half_groups):
                send_r[first // gc + part, :, 0 : flat + flat_e] = value[
                    part * gc : (part + 1) * gc
                ].astype(jnp.bfloat16)
        if turn == 0:
            with jax.named_scope("barrier"):
                pl.semaphore_wait(barrier, groups)
        with jax.named_scope("start_r"):
            if turn == 0:
                order = [(plane, n) for n in range(2) for plane in (far_a, far_b)]
            else:
                order = [(py, n) for n in range(1, along_z)]
                order += [(sibling, 0), (sibling, 1)]
                order += [(plane, n) for n in range(2, along_z) for plane in (far_a, far_b, sibling)]
            for plane, n in order:
                copy_r(to(plane, n), me).start()
    recv_r[me] = send_r[me]

    for turn in range(2):
        first = (1 - side if turn == 0 else side) * half
        with jax.named_scope(f"gated_l{turn}"):
            value = gated(0, first, 0, flat_m)
            for part in range(half_groups):
                send_l[first // gc + part] = value[part * gc : (part + 1) * gc].astype(jnp.bfloat16)
        with jax.named_scope("start_l"):
            if turn == 0:
                order = [(plane, n) for n in range(2) for plane in (far_a, far_b)]
            else:
                order = [(py, n) for n in range(1, along_z)]
                order += [(sibling, 0), (sibling, 1)]
                order += [(plane, n) for n in range(2, along_z) for plane in (far_a, far_b, sibling)]
            for plane, n in order:
                copy_l(to(plane, n), me, n).start()
    recv_l[me] = send_l[me]

    with jax.named_scope("gate"):
        loads[3].wait()
        loads[4].wait()
        gate_f32[...] = 0.5 + 0.5 * jnp.tanh(
            0.5 * jnp.dot(normed_bf[...], gate_ref[...], preferred_element_type=jnp.float32)
        )

    lane8 = lax.broadcasted_iota(jnp.int32, (gc, LANES), 1)

    def lanes_from(value, start):
        block = value[:, start // LANES * LANES : start // LANES * LANES + LANES]
        shift = start % LANES
        return block if shift == 0 else pltpu.roll(block, LANES - shift, 1)

    def spread_main(value, s, target):
        for k in range(cols):
            at = pl.multiple_of((s * cols + k) * gc, gc)
            target[pl.ds(at, gc), :] = lanes_from(value, k * main)

    def spread_edge(value, s):
        for k in range(cols):
            at = pl.multiple_of((s * cols + k) * gc, gc)
            edge_s[pl.ds(at, gc), :] = lanes_from(value, flat + k * edge)

    def spread_right(value, s, target):
        for k in range(cols):
            at = pl.multiple_of((s * cols + k) * gc, gc)
            begin = flat_m + k * edge
            block = value[:, begin // LANES * LANES : begin // LANES * LANES + LANES]
            shift = (main - begin) % LANES
            block = block if shift == 0 else pltpu.roll(block, shift, 1)
            target[pl.ds(at, gc), :] = jnp.where(lane8 < main, lanes_from(value, k * main), block)

    planes = (py, far_a, far_b, sibling)

    def take_r(n, carry):
        for plane in planes:
            s = source(plane, n)

            @pl.when(s != me)
            def _():
                copy_r(s, s).wait_recv()

            copy_x(s).start()
        for plane in planes:
            s = source(plane, n)
            value = recv_r[s].astype(jnp.float32)
            spread_right(value, s, right_s.at[px])
            spread_edge(value, s)
        return carry

    with jax.named_scope("take_r"):
        lax.fori_loop(0, along_z, take_r, 0)

    def take_x(n, carry):
        pltpu.make_async_remote_copy(
            src_ref=recv_r.at[0:along_y, :, 0:wide], dst_ref=recv_x.at[0:along_y],
            send_sem=send_sem.at[1], recv_sem=rsem_x.at[n], device_id=partner,
            device_id_type=MESH,
        ).wait_recv()
        for plane in planes:
            s = source(plane, n)
            spread_right(recv_x[s].astype(jnp.float32), s, right_s.at[1 - px])
        return carry

    with jax.named_scope("take_x"):
        lax.fori_loop(0, along_z, take_x, 0)

    def tri(left, width, c, first):
        for h in range(2):
            if first:
                right = right_s[h, pl.ds(c, residues, stride=gc), :].astype(jnp.bfloat16)
                right_bf[h, c] = right
            else:
                right = right_bf[h, c]
            block = lax.dot_general(
                right[:, 0:rows], left[:, 0:width], (((0,), (0,)), ((), ())),
                preferred_element_type=jnp.float32,
            )
            tri_s[pl.ds(h * rows * gc + c, rows, stride=gc), 0:width] = block

    def pack(d, width):
        pieces = []
        per = LANES // width
        for begin in range(0, cols, per):
            total = None
            for n in range(min(per, cols - begin)):
                at = pl.multiple_of((d * cols + begin + n) * gc, gc)
                piece = tri_s[pl.ds(at, gc), :]
                piece = piece if n == 0 else pltpu.roll(piece, n * width, 1)
                total = piece if n == 0 else jnp.where(lane8 < n * width, total, piece)
            pieces.append(total)
        return jnp.concatenate(pieces, axis=1).astype(jnp.bfloat16)

    def ship(width, buffer, landed, copy):
        def around(n, carry):
            goals = [to(plane, n) for plane in (far_a, far_b, sibling, py)]
            packed = [pack(d, width) for d in goals]
            for d, value in zip(goals, packed):
                buffer[d] = value
            for d in goals:

                @pl.when(d != me)
                def _():
                    copy(d, me).start()

            return carry

        lax.fori_loop(0, along_z, around, 0)
        landed[me] = buffer[me]

    with jax.named_scope("tri_e"):
        for c in range(gc):
            left = edge_s[pl.ds(c, residues, stride=gc), :].astype(jnp.bfloat16)
            tri(left, edge, c, True)
    with jax.named_scope("ship_e"):
        ship(edge, send_e, recv_e, copy_e)

    def take_l(n, carry):
        @pl.when(n == 0)
        def _():
            copy_l(0, 0, 0, along_y - 1).wait_recv()

        @pl.when(n > 0)
        def _():
            copy_l(0, 0, n, along_y).wait_recv()

        for plane in planes:
            s = source(plane, n)
            spread_main(recv_l[s].astype(jnp.float32), s, left_s)
        return carry

    with jax.named_scope("take_l"):
        lax.fori_loop(0, along_z, take_l, 0)
    with jax.named_scope("tri_m"):
        for c in range(gc):
            left = left_s[pl.ds(c, residues, stride=gc), :].astype(jnp.bfloat16)
            tri(left, main, c, False)
    with jax.named_scope("ship_m"):
        ship(main, send_b, recv_b, copy_b)

    def final(received, low, width):
        count = width * cols
        triangle = received[:, :, 0:count].astype(jnp.float32).reshape(hidden, count)
        normed_tri = layer_norm_lead(triangle).astype(jnp.bfloat16)
        mixed = lax.dot_general(
            normed_tri, out_w_ref[...], (((0,), (0,)), ((), ())),
            preferred_element_type=jnp.float32,
        )
        first = 0 if low == 0 else flat_m
        update = (gate_f32[first : first + count] * mixed).astype(jnp.bfloat16)
        for j in range(cols):
            out_ref[j, low : low + width] = update[j * width : (j + 1) * width]

    with jax.named_scope("take_e"):
        copy_e(0, 0, groups - 1).wait_recv()
    with jax.named_scope("final_e"):
        final(recv_e, main, edge)
    with jax.named_scope("finish"):
        pltpu.make_async_remote_copy(
            src_ref=send_r.at[0 : groups - 1], dst_ref=recv_r.at[0 : groups - 1],
            send_sem=send_sem.at[0], recv_sem=rsem_r.at[0], device_id=partner,
            device_id_type=MESH,
        ).wait_send()
        copy_x(0, groups).wait_send()
        copy_l(0, 0, 0, groups - 1).wait_send()
        copy_e(0, 0, groups - 1).wait_send()
    with jax.named_scope("take_b"):
        copy_b(0, 0, groups - 1).wait_recv()
    with jax.named_scope("final_m"):
        final(recv_b, 0, main)
    with jax.named_scope("finish_b"):
        copy_b(0, 0, groups - 1).wait_send()


def scratch_list(main, rows, cols, chans, hidden, groups, residues):
    gc = hidden // groups
    flat_m, flat_e = main * cols, (rows - main) * cols
    wide = up(flat_m + flat_e, LANES)
    both = up(flat_m + 2 * flat_e, LANES)
    bf, f32 = jnp.bfloat16, jnp.float32
    return [
        ((cols, rows, chans), bf),
        ((1, residues), jnp.int32),
        ((chans, 4 * hidden), bf),
        ((chans, chans), bf),
        ((hidden, chans), bf),
        ((4 * hidden, chans), bf),
        ((rows * cols, chans), bf),
        ((rows * cols, chans), bf),
        ((rows * cols, chans), f32),
        ((groups, gc, both), bf),
        ((groups, gc, both), bf),
        ((groups, gc, wide), bf),
        ((groups, gc, flat_m), bf),
        ((groups, gc, flat_m), bf),
        ((residues * gc, LANES), f32),
        ((residues * gc, LANES), f32),
        ((2, residues * gc, LANES), f32),
        ((2, gc, residues, LANES), bf),
        ((residues * gc, LANES), f32),
        ((groups, gc, up(flat_e, LANES)), bf),
        ((groups, gc, up(flat_e, LANES)), bf),
        ((groups, gc, flat_m), bf),
        ((groups, gc, flat_m), bf),
    ]


def fits_kernel(sizes, rows, cols, chans, hidden, residues):
    groups = sizes["gy"] * sizes["gz"]
    main = rows // HALF_LANES * HALF_LANES
    edge = rows - main
    if sizes["gx"] != 2 or hidden % (4 * groups) or hidden // groups != 8:
        return False
    if sizes["gy"] != 4 or residues != 2 * rows or residues != groups * cols:
        return False
    if chans != LANES or main != HALF_LANES or edge != 16 or cols % 2:
        return False
    total = 0
    for shape, kind in scratch_list(main, rows, cols, chans, hidden, groups, residues):
        count = 1
        for extent in shape:
            count *= extent
        total += count * jnp.dtype(kind).itemsize
    return total < VMEM_BUDGET // 3


def local_fused(sizes, pair_map, residue_mask, proj_weight, gate_weight, out_weight):
    rows, cols, chans = pair_map.shape
    hidden = out_weight.shape[0]
    residues = residue_mask.shape[0]
    if not fits_kernel(sizes, rows, cols, chans, hidden, residues):
        return local(pair_map, residue_mask, proj_weight, gate_weight, out_weight)
    groups = sizes["gy"] * sizes["gz"]
    main = rows // HALF_LANES * HALF_LANES
    dma = pltpu.SemaphoreType.DMA
    vmem = pl.BlockSpec(memory_space=pltpu.VMEM)
    turned = pl.pallas_call(
        functools.partial(fused_kernel, sizes["gy"], sizes["gz"], main),
        out_shape=pltpu.VMEM((cols, rows, chans), jnp.bfloat16),
        in_specs=[pl.BlockSpec(memory_space=pltpu.HBM)] * 5,
        out_specs=vmem,
        scratch_shapes=[
            pltpu.VMEM(shape, kind)
            for shape, kind in scratch_list(main, rows, cols, chans, hidden, groups, residues)
        ]
        + [dma((5,)), dma((5,)), dma((groups,)), dma((sizes["gz"],)), dma((sizes["gz"],)), dma((2,))],
        compiler_params=pltpu.CompilerParams(
            collective_id=0, has_side_effects=True, vmem_limit_bytes=VMEM_ALL - 204800
        ),
    )(
        pair_map.transpose(1, 0, 2), residue_mask.reshape(1, residues),
        proj_weight, gate_weight, out_weight,
    )
    return turned.transpose(1, 0, 2)


def solution(mesh):
    placed = (P("gx", ("gy", "gz"), None), P(), P(), P(), P())
    return jax.shard_map(
        functools.partial(local_fused, dict(mesh.shape)), mesh=mesh, in_specs=placed, out_specs=P("gx", ("gy", "gz"), None), check_vma=False
    )
```

time: 29.4 us -> 28.1 us (0.956)
  local copies, waits for them, and re-layouts: 1.62 us -> 0.68 us
  Pallas kernels: 27.6 us -> 27.3 us
    unnamed x1, local copies, waits for them, and re-layouts: 1.62 us -> 0.68 us
    pallas_call x1, Pallas kernels: 27.6 us -> 27.3 us  [local_fused(): pl.pallas_call(functools.partial(fused_kernel, sizes['gy'], sizes['gz'],...]
where the time goes in v1:
time: 28.1 us; the launch traced here: 28 us
  Pallas kernels  27.3 us (97%)
  local copies, waits for them, and re-layouts  0.68 us (2%)
    pallas_call x1, Pallas kernels, local_fused(): pl.pallas_call(functools.partial(fused_kernel, sizes['gy'], sizes['gz'],...  27.3 us
    unnamed x1, local copies, waits for them, and re-layouts  0.68 us

profile of v1, /device:TPU:0, one launch (start us, length us, event | category | flops | bytes accessed | tf_op | source)
XLA Modules:
  0.0 28.0 jit_solution(14606920575114831522)
XLA Ops:
  0.0 27.3 %shard_map.55 = bf16[10,80,128]{2,1,0:T(8,128)(2,1)S(1)} custom-call(bf16[10,80,128]{2,1,0:T(8,128)(2,1)} %bitcast.4, s32[1,160]{1,0:T(1,128)} %bitcast.5, bf16[128,512]{1,0:T(8,128)(2,1)} %proj_hbm.1, bf16[128,128]{1,0:T(8,128)(2,1)} %gate_hbm.1, bf16[128,128]{1,0:T(8,128)(2,1)} %out_w_hbm.1), custom_call_target="tpu_custom_call" | custom-call | tf_op jit(solution)/shard_map/pallas_call | solution.py:551
  27.3 0.7 %copy.7 = bf16[80,10,128]{2,0,1:T(8,128)(2,1)} copy(bf16[80,10,128]{2,0,1:T(8,128)(2,1)S(1)} %bitcast.3) | data formatting | bytes 409600

commit v2 on v1

--- a/solution.py
+++ b/solution.py
@@ -148,7 +148,7 @@
     pair_hbm, mask_hbm, proj_hbm, gate_hbm, out_w_hbm, out_ref,
     pair_ref, mask_ref, proj_ref, gate_ref, out_w_ref,
     proj_s, normed_bf, masked_bf, gate_f32, send_r, recv_r, recv_x, send_l, recv_l,
-    left_s, edge_s, right_s, right_bf, tri_s, send_e, recv_e, send_b, recv_b,
+    left_s, edge_s, edge_bf, right_s, right_bf, tri_s, send_e, recv_e, send_b, recv_b,
     load_sem, send_sem, rsem_r, rsem_x, rsem_l, rsem_b,
 ):
     cols, rows, chans = pair_ref.shape
@@ -159,6 +159,7 @@
     flat_m, flat_e = main * cols, edge * cols
     flat = flat_m + flat_e
     wide = up(flat, LANES)
+    both = up(flat + flat_e, LANES)
     residues = mask_ref.shape[1]
     px, py, pz = lax.axis_index("gx"), lax.axis_index("gy"), lax.axis_index("gz")
     me = py * along_z + pz
@@ -228,23 +229,32 @@
     half_groups = groups // 2
 
     def gated(base, first, low, high):
-        both = jnp.concatenate(
+        rows_of = jnp.concatenate(
             [
                 proj_s[pl.ds(pl.multiple_of(base + first, half), half), :],
                 proj_s[pl.ds(pl.multiple_of(base + hidden + first, half), half), :],
             ],
             axis=0,
         )
-        both = lax.dot_general(
-            both, masked_bf[low:high, :], (((1,), (1,)), ((), ())),
+        value = lax.dot_general(
+            rows_of, masked_bf[low:high, :], (((1,), (1,)), ((), ())),
             preferred_element_type=jnp.float32,
         )
-        return gate_by(both[0:half], both[half:])
+        return gate_by(value[0:half], value[half:])
 
     def copy_r(d, slot):
         return pltpu.make_async_remote_copy(
-            src_ref=send_r.at[d], dst_ref=recv_r.at[slot], send_sem=send_sem.at[0],
-            recv_sem=rsem_r.at[slot], device_id=place(d), device_id_type=MESH,
+            src_ref=send_r.at[d, :, 0:wide], dst_ref=recv_r.at[slot, :, 0:wide],
+            send_sem=send_sem.at[0], recv_sem=rsem_r.at[slot], device_id=place(d),
+            device_id_type=MESH,
+        )
+
+    def copy_rest(d, slot, n, count=1):
+        return pltpu.make_async_remote_copy(
+            src_ref=send_r.at[pl.ds(d, count), :, wide:both],
+            dst_ref=recv_r.at[pl.ds(slot, count), :, wide:both],
+            send_sem=send_sem.at[5], recv_sem=rsem_l.at[n + along_z], device_id=place(d),
+            device_id_type=MESH,
         )
 
     def copy_x(s, count=1):
@@ -292,6 +302,12 @@
                 order += [(plane, n) for n in range(2, along_z) for plane in (far_a, far_b, sibling)]
             for plane, n in order:
                 copy_r(to(plane, n), me).start()
+            if turn == 1:
+                for n in range(along_z):
+                    for plane in (far_a, far_b, sibling, py):
+                        if n == 0 and plane is py:
+                            continue
+                        copy_rest(to(plane, n), me, n).start()
     recv_r[me] = send_r[me]
 
     for turn in range(2):
@@ -300,15 +316,6 @@
             value = gated(0, first, 0, flat_m)
             for part in range(half_groups):
                 send_l[first // gc + part] = value[part * gc : (part + 1) * gc].astype(jnp.bfloat16)
-        with jax.named_scope("start_l"):
-            if turn == 0:
-                order = [(plane, n) for n in range(2) for plane in (far_a, far_b)]
-            else:
-                order = [(py, n) for n in range(1, along_z)]
-                order += [(sibling, 0), (sibling, 1)]
-                order += [(plane, n) for n in range(2, along_z) for plane in (far_a, far_b, sibling)]
-            for plane, n in order:
-                copy_l(to(plane, n), me, n).start()
     recv_l[me] = send_l[me]
 
     with jax.named_scope("gate"):
@@ -329,11 +336,6 @@
         for k in range(cols):
             at = pl.multiple_of((s * cols + k) * gc, gc)
             target[pl.ds(at, gc), :] = lanes_from(value, k * main)
-
-    def spread_edge(value, s):
-        for k in range(cols):
-            at = pl.multiple_of((s * cols + k) * gc, gc)
-            edge_s[pl.ds(at, gc), :] = lanes_from(value, flat + k * edge)
 
     def spread_right(value, s, target):
         for k in range(cols):
@@ -346,24 +348,84 @@
 
     planes = (py, far_a, far_b, sibling)
 
+    def forward(s):
+        @pl.when(s != me)
+        def _():
+            copy_r(s, s).wait_recv()
+
+        copy_x(s).start()
+
+    def spread_r(s):
+        value = recv_r[s, :, 0:wide].astype(jnp.float32)
+        spread_right(value, s, right_s.at[px])
+
     def take_r(n, carry):
+        for plane in planes[1:]:
+            forward(source(plane, n))
+        for plane in planes[1:]:
+            spread_r(source(plane, n))
+        return carry
+
+    def start_l(n, carry):
+        for plane in (far_a, far_b, sibling, py):
+            d = to(plane, n)
+
+            @pl.when(d != me)
+            def _():
+                copy_l(d, me, n).start()
+
+        return carry
+
+    with jax.named_scope("take_own"):
+        for n in range(along_z):
+            forward(source(py, n))
+        for n in range(along_z):
+            spread_r(source(py, n))
+    with jax.named_scope("take_r"):
+        lax.fori_loop(0, 2, take_r, 0)
+    with jax.named_scope("start_l"):
+        lax.fori_loop(0, along_z, start_l, 0)
+    with jax.named_scope("take_r"):
+        lax.fori_loop(2, along_z, take_r, 0)
+
+    def take_rest(n, carry):
+        @pl.when(n == 0)
+        def _():
+            copy_rest(0, 0, 0, along_y - 1).wait_recv()
+
+        @pl.when(n > 0)
+        def _():
+            copy_rest(0, 0, n, along_y).wait_recv()
+
         for plane in planes:
             s = source(plane, n)
-
-            @pl.when(s != me)
-            def _():
-                copy_r(s, s).wait_recv()
-
-            copy_x(s).start()
-        for plane in planes:
-            s = source(plane, n)
-            value = recv_r[s].astype(jnp.float32)
-            spread_right(value, s, right_s.at[px])
-            spread_edge(value, s)
+            value = recv_r[s, :, flat_m:both].astype(jnp.float32)
+            for k in range(cols):
+                at = pl.multiple_of((s * cols + k) * gc, gc)
+                edge_s[pl.ds(at, gc), :] = lanes_from(value, flat_e + k * edge)
         return carry
 
-    with jax.named_scope("take_r"):
-        lax.fori_loop(0, along_z, take_r, 0)
+    with jax.named_scope("take_rest"):
+        lax.fori_loop(0, along_z, take_rest, 0)
+
+    def tri(left, width, c, h, first):
+        if first:
+            right = right_s[h, pl.ds(c, residues, stride=gc), :].astype(jnp.bfloat16)
+            right_bf[h, c] = right
+        else:
+            right = right_bf[h, c]
+        block = lax.dot_general(
+            right[:, 0:rows], left[:, 0:width], (((0,), (0,)), ((), ())),
+            preferred_element_type=jnp.float32,
+        )
+        at = pl.multiple_of(h * rows * gc, gc)
+        tri_s[pl.ds(at + c, rows, stride=gc), 0:width] = block
+
+    with jax.named_scope("tri_own"):
+        for c in range(gc):
+            left = edge_s[pl.ds(c, residues, stride=gc), :].astype(jnp.bfloat16)
+            edge_bf[c] = left
+            tri(left, edge, c, px, True)
 
     def take_x(n, carry):
         pltpu.make_async_remote_copy(
@@ -378,19 +440,6 @@
 
     with jax.named_scope("take_x"):
         lax.fori_loop(0, along_z, take_x, 0)
-
-    def tri(left, width, c, first):
-        for h in range(2):
-            if first:
-                right = right_s[h, pl.ds(c, residues, stride=gc), :].astype(jnp.bfloat16)
-                right_bf[h, c] = right
-            else:
-                right = right_bf[h, c]
-            block = lax.dot_general(
-                right[:, 0:rows], left[:, 0:width], (((0,), (0,)), ((), ())),
-                preferred_element_type=jnp.float32,
-            )
-            tri_s[pl.ds(h * rows * gc + c, rows, stride=gc), 0:width] = block
 
     def pack(d, width):
         pieces = []
@@ -424,8 +473,7 @@
 
     with jax.named_scope("tri_e"):
         for c in range(gc):
-            left = edge_s[pl.ds(c, residues, stride=gc), :].astype(jnp.bfloat16)
-            tri(left, edge, c, True)
+            tri(edge_bf[c], edge, c, 1 - px, True)
     with jax.named_scope("ship_e"):
         ship(edge, send_e, recv_e, copy_e)
 
@@ -448,7 +496,8 @@
     with jax.named_scope("tri_m"):
         for c in range(gc):
             left = left_s[pl.ds(c, residues, stride=gc), :].astype(jnp.bfloat16)
-            tri(left, main, c, False)
+            for h in range(2):
+                tri(left, main, c, h, False)
     with jax.named_scope("ship_m"):
         ship(main, send_b, recv_b, copy_b)
 
@@ -471,10 +520,12 @@
         final(recv_e, main, edge)
     with jax.named_scope("finish"):
         pltpu.make_async_remote_copy(
-            src_ref=send_r.at[0 : groups - 1], dst_ref=recv_r.at[0 : groups - 1],
+            src_ref=send_r.at[0 : groups - 1, :, 0:wide],
+            dst_ref=recv_r.at[0 : groups - 1, :, 0:wide],
             send_sem=send_sem.at[0], recv_sem=rsem_r.at[0], device_id=partner,
             device_id_type=MESH,
         ).wait_send()
+        copy_rest(0, 0, 0, groups - 1).wait_send()
         copy_x(0, groups).wait_send()
         copy_l(0, 0, 0, groups - 1).wait_send()
         copy_e(0, 0, groups - 1).wait_send()
@@ -509,6 +560,7 @@
         ((groups, gc, flat_m), bf),
         ((residues * gc, LANES), f32),
         ((residues * gc, LANES), f32),
+        ((gc, residues, LANES), bf),
         ((2, residues * gc, LANES), f32),
         ((2, gc, residues, LANES), bf),
         ((residues * gc, LANES), f32),
@@ -557,7 +609,7 @@
             pltpu.VMEM(shape, kind)
             for shape, kind in scratch_list(main, rows, cols, chans, hidden, groups, residues)
         ]
-        + [dma((5,)), dma((5,)), dma((groups,)), dma((sizes["gz"],)), dma((sizes["gz"],)), dma((2,))],
+        + [dma((5,)), dma((6,)), dma((groups,)), dma((sizes["gz"],)), dma((2 * sizes["gz"],)), dma((2,))],
         compiler_params=pltpu.CompilerParams(
             collective_id=0, has_side_effects=True, vmem_limit_bytes=VMEM_ALL - 204800
         ),

time: 28.1 us -> 26.3 us (0.936)
  Pallas kernels: 27.3 us -> 25.5 us
    pallas_call x1, Pallas kernels: 27.3 us -> 25.5 us  [local_fused(): pl.pallas_call(functools.partial(fused_kernel, sizes['gy'], sizes['gz'],...]
where the time goes in v2:
time: 26.3 us; the launch traced here: 26.2 us
  Pallas kernels  25.5 us (97%)
  local copies, waits for them, and re-layouts  0.68 us (3%)
    pallas_call x1, Pallas kernels, local_fused(): pl.pallas_call(functools.partial(fused_kernel, sizes['gy'], sizes['gz'],...  25.5 us
    unnamed x1, local copies, waits for them, and re-layouts  0.68 us

profile of v2, /device:TPU:0, one launch (start us, length us, event | category | flops | bytes accessed | tf_op | source)
XLA Modules:
  0.0 26.2 jit_solution(10581893945147355663)
XLA Ops:
  0.0 25.5 %shard_map.55 = bf16[10,80,128]{2,1,0:T(8,128)(2,1)S(1)} custom-call(bf16[10,80,128]{2,1,0:T(8,128)(2,1)} %bitcast.4, s32[1,160]{1,0:T(1,128)} %bitcast.5, bf16[128,512]{1,0:T(8,128)(2,1)} %proj_hbm.1, bf16[128,128]{1,0:T(8,128)(2,1)} %gate_hbm.1, bf16[128,128]{1,0:T(8,128)(2,1)} %out_w_hbm.1), custom_call_target="tpu_custom_call" | custom-call | tf_op jit(solution)/shard_map/pallas_call | solution.py:603
  25.5 0.7 %copy.7 = bf16[80,10,128]{2,0,1:T(8,128)(2,1)} copy(bf16[80,10,128]{2,0,1:T(8,128)(2,1)S(1)} %bitcast.3) | data formatting | bytes 409600

commit v3 on v2

--- a/solution.py
+++ b/solution.py
@@ -130,13 +130,16 @@
 
 MESH = pl.DeviceIdType.MESH
 LANES = 128
-HALF_LANES = 64
 VMEM_ALL = 67043328
 VMEM_BUDGET = 48 * 2**20
 
 
 def up(value, step):
     return -(-value // step) * step
+
+
+def main_rows(rows):
+    return rows * 8 // 10 // 16 * 16
 
 
 def gate_by(gate, value):
@@ -169,17 +172,13 @@
     def place(d):
         return (px, d // along_z, d % along_z)
 
-    far_a, far_b = (1 - side) * middle, (1 - side) * middle + 1
+    far_a = (1 - side) * (along_y - 1)
+    far_b = side * (middle - 1) + (1 - side) * middle
     sibling = side * middle + (py + 1) % middle
 
     def to(plane, n):
-        return plane * along_z + (pz + n) % along_z
-
-    def source(plane, n):
-        return plane * along_z + (pz + along_z - n) % along_z
-
-    def turn_of(s):
-        return (pz + along_z - s % along_z) % along_z
+        m = n if plane is py else (n + 2) % along_z
+        return plane * along_z + (pz // 2 + m // 2) % (along_z // 2) * 2 + (pz + m) % 2
 
     partner = (1 - px, py, pz)
     barrier = pltpu.get_barrier_semaphore()
@@ -257,10 +256,10 @@
             device_id_type=MESH,
         )
 
-    def copy_x(s, count=1):
+    def copy_x(s, n, count=1):
         return pltpu.make_async_remote_copy(
             src_ref=recv_r.at[pl.ds(s, count), :, 0:wide], dst_ref=recv_x.at[pl.ds(s, count)],
-            send_sem=send_sem.at[1], recv_sem=rsem_x.at[turn_of(s)],
+            send_sem=send_sem.at[1], recv_sem=rsem_x.at[n],
             device_id=partner, device_id_type=MESH,
         )
 
@@ -298,8 +297,8 @@
                 order = [(plane, n) for n in range(2) for plane in (far_a, far_b)]
             else:
                 order = [(py, n) for n in range(1, along_z)]
-                order += [(sibling, 0), (sibling, 1)]
-                order += [(plane, n) for n in range(2, along_z) for plane in (far_a, far_b, sibling)]
+                order += [(sibling, n) for n in range(along_z)]
+                order += [(plane, n) for n in range(2, along_z) for plane in (far_a, far_b)]
             for plane, n in order:
                 copy_r(to(plane, n), me).start()
             if turn == 1:
@@ -315,7 +314,9 @@
         with jax.named_scope(f"gated_l{turn}"):
             value = gated(0, first, 0, flat_m)
             for part in range(half_groups):
-                send_l[first // gc + part] = value[part * gc : (part + 1) * gc].astype(jnp.bfloat16)
+                send_l[first // gc + part, :, 0:flat_m] = value[
+                    part * gc : (part + 1) * gc
+                ].astype(jnp.bfloat16)
     recv_l[me] = send_l[me]
 
     with jax.named_scope("gate"):
@@ -327,43 +328,54 @@
 
     lane8 = lax.broadcasted_iota(jnp.int32, (gc, LANES), 1)
 
-    def lanes_from(value, start):
-        block = value[:, start // LANES * LANES : start // LANES * LANES + LANES]
-        shift = start % LANES
-        return block if shift == 0 else pltpu.roll(block, LANES - shift, 1)
+    def lift(value, begin, width, lane):
+        low, high = begin // LANES, (begin + width - 1) // LANES
+        shift = (lane - begin) % LANES
+
+        def turned(n):
+            block = value[:, n * LANES : (n + 1) * LANES]
+            return block if shift == 0 else pltpu.roll(block, shift, 1)
+
+        if low == high:
+            return turned(low)
+        return jnp.where(lane8 < lane + high * LANES - begin, turned(low), turned(high))
 
     def spread_main(value, s, target):
         for k in range(cols):
             at = pl.multiple_of((s * cols + k) * gc, gc)
-            target[pl.ds(at, gc), :] = lanes_from(value, k * main)
+            target[pl.ds(at, gc), :] = lift(value, k * main, main, 0)
 
     def spread_right(value, s, target):
         for k in range(cols):
             at = pl.multiple_of((s * cols + k) * gc, gc)
-            begin = flat_m + k * edge
-            block = value[:, begin // LANES * LANES : begin // LANES * LANES + LANES]
-            shift = (main - begin) % LANES
-            block = block if shift == 0 else pltpu.roll(block, shift, 1)
-            target[pl.ds(at, gc), :] = jnp.where(lane8 < main, lanes_from(value, k * main), block)
+            target[pl.ds(at, gc), :] = jnp.where(
+                lane8 < main,
+                lift(value, k * main, main, 0),
+                lift(value, flat_m + k * edge, edge, main),
+            )
 
     planes = (py, far_a, far_b, sibling)
 
-    def forward(s):
-        @pl.when(s != me)
-        def _():
-            copy_r(s, s).wait_recv()
-
-        copy_x(s).start()
+    def forward(plane, n):
+        s = to(plane, n)
+        copy_r(s, s).wait_recv()
+        copy_x(s, n).start()
 
     def spread_r(s):
         value = recv_r[s, :, 0:wide].astype(jnp.float32)
         spread_right(value, s, right_s.at[px])
 
-    def take_r(n, carry):
-        for plane in planes[1:]:
-            forward(source(plane, n))
-        for plane in planes[1:]:
-            spread_r(source(plane, n))
+    def take_plane(plane, first):
+        for n in range(first, along_z):
+            forward(plane, n)
+        for n in range(along_z):
+            spread_r(to(plane, n))
+
+    def take_far(n, carry):
+        for plane in (far_a, far_b):
+            forward(plane, n)
+        for plane in (far_a, far_b):
+            spread_r(to(plane, n))
         return carry
 
     def start_l(n, carry):
@@ -376,17 +388,30 @@
 
         return carry
 
+    copy_x(me, 0).start()
     with jax.named_scope("take_own"):
-        for n in range(along_z):
-            forward(source(py, n))
-        for n in range(along_z):
-            spread_r(source(py, n))
-    with jax.named_scope("take_r"):
-        lax.fori_loop(0, 2, take_r, 0)
+        take_plane(py, 1)
+    with jax.named_scope("take_far0"):
+        take_far(0, 0)
+    with jax.named_scope("take_sib"):
+        take_plane(sibling, 0)
+    with jax.named_scope("take_far1"):
+        take_far(1, 0)
+    with jax.named_scope("wait_send"):
+        pltpu.make_async_remote_copy(
+            src_ref=send_r.at[0 : groups - 1, :, 0:wide],
+            dst_ref=recv_r.at[0 : groups - 1, :, 0:wide],
+            send_sem=send_sem.at[0], recv_sem=rsem_r.at[0], device_id=partner,
+            device_id_type=MESH,
+        ).wait_send()
     with jax.named_scope("start_l"):
         lax.fori_loop(0, along_z, start_l, 0)
-    with jax.named_scope("take_r"):
-        lax.fori_loop(2, along_z, take_r, 0)
+    with jax.named_scope("take_far2"):
+        take_far(2, 0)
+    with jax.named_scope("take_far3"):
+        take_far(3, 0)
+
+    rest_low = flat // LANES * LANES
 
     def take_rest(n, carry):
         @pl.when(n == 0)
@@ -398,11 +423,11 @@
             copy_rest(0, 0, n, along_y).wait_recv()
 
         for plane in planes:
-            s = source(plane, n)
-            value = recv_r[s, :, flat_m:both].astype(jnp.float32)
+            s = to(plane, n)
+            value = recv_r[s, :, rest_low:both].astype(jnp.float32)
             for k in range(cols):
                 at = pl.multiple_of((s * cols + k) * gc, gc)
-                edge_s[pl.ds(at, gc), :] = lanes_from(value, flat_e + k * edge)
+                edge_s[pl.ds(at, gc), :] = lift(value, flat + k * edge - rest_low, edge, 0)
         return carry
 
     with jax.named_scope("take_rest"):
@@ -434,7 +459,7 @@
             device_id_type=MESH,
         ).wait_recv()
         for plane in planes:
-            s = source(plane, n)
+            s = to(plane, n)
             spread_right(recv_x[s].astype(jnp.float32), s, right_s.at[1 - px])
         return carry
 
@@ -442,17 +467,17 @@
         lax.fori_loop(0, along_z, take_x, 0)
 
     def pack(d, width):
-        pieces = []
-        per = LANES // width
-        for begin in range(0, cols, per):
-            total = None
-            for n in range(min(per, cols - begin)):
-                at = pl.multiple_of((d * cols + begin + n) * gc, gc)
-                piece = tri_s[pl.ds(at, gc), :]
-                piece = piece if n == 0 else pltpu.roll(piece, n * width, 1)
-                total = piece if n == 0 else jnp.where(lane8 < n * width, total, piece)
-            pieces.append(total)
-        return jnp.concatenate(pieces, axis=1).astype(jnp.bfloat16)
+        blocks = [None] * (up(cols * width, LANES) // LANES)
+        for j in range(cols):
+            at = pl.multiple_of((d * cols + j) * gc, gc)
+            shift = j * width % LANES
+            piece = tri_s[pl.ds(at, gc), :]
+            piece = piece if shift == 0 else pltpu.roll(piece, shift, 1)
+            n = j * width // LANES
+            blocks[n] = piece if shift == 0 else jnp.where(lane8 < shift, blocks[n], piece)
+            if shift + width > LANES:
+                blocks[n + 1] = piece
+        return jnp.concatenate(blocks, axis=1).astype(jnp.bfloat16)
 
     def ship(width, buffer, landed, copy):
         def around(n, carry):
@@ -487,7 +512,7 @@
             copy_l(0, 0, n, along_y).wait_recv()
 
         for plane in planes:
-            s = source(plane, n)
+            s = to(plane, n)
             spread_main(recv_l[s].astype(jnp.float32), s, left_s)
         return carry
 
@@ -519,14 +544,8 @@
     with jax.named_scope("final_e"):
         final(recv_e, main, edge)
     with jax.named_scope("finish"):
-        pltpu.make_async_remote_copy(
-            src_ref=send_r.at[0 : groups - 1, :, 0:wide],
-            dst_ref=recv_r.at[0 : groups - 1, :, 0:wide],
-            send_sem=send_sem.at[0], recv_sem=rsem_r.at[0], device_id=partner,
-            device_id_type=MESH,
-        ).wait_send()
         copy_rest(0, 0, 0, groups - 1).wait_send()
-        copy_x(0, groups).wait_send()
+        copy_x(0, 0, groups).wait_send()
         copy_l(0, 0, 0, groups - 1).wait_send()
         copy_e(0, 0, groups - 1).wait_send()
     with jax.named_scope("take_b"):
@@ -556,8 +575,8 @@
         ((groups, gc, both), bf),
         ((groups, gc, both), bf),
         ((groups, gc, wide), bf),
-        ((groups, gc, flat_m), bf),
-        ((groups, gc, flat_m), bf),
+        ((groups, gc, up(flat_m, LANES)), bf),
+        ((groups, gc, up(flat_m, LANES)), bf),
         ((residues * gc, LANES), f32),
         ((residues * gc, LANES), f32),
         ((gc, residues, LANES), bf),
@@ -566,20 +585,20 @@
         ((residues * gc, LANES), f32),
         ((groups, gc, up(flat_e, LANES)), bf),
         ((groups, gc, up(flat_e, LANES)), bf),
-        ((groups, gc, flat_m), bf),
-        ((groups, gc, flat_m), bf),
+        ((groups, gc, up(flat_m, LANES)), bf),
+        ((groups, gc, up(flat_m, LANES)), bf),
     ]
 
 
 def fits_kernel(sizes, rows, cols, chans, hidden, residues):
     groups = sizes["gy"] * sizes["gz"]
-    main = rows // HALF_LANES * HALF_LANES
+    main = main_rows(rows)
     edge = rows - main
     if sizes["gx"] != 2 or hidden % (4 * groups) or hidden // groups != 8:
         return False
-    if sizes["gy"] != 4 or residues != 2 * rows or residues != groups * cols:
+    if sizes["gy"] != 4 or sizes["gz"] != 4 or residues != 2 * rows or residues != groups * cols:
         return False
-    if chans != LANES or main != HALF_LANES or edge != 16 or cols % 2:
+    if chans != LANES or rows > LANES or rows % 16 or main < 16 or edge < 16:
         return False
     total = 0
     for shape, kind in scratch_list(main, rows, cols, chans, hidden, groups, residues):
@@ -597,7 +616,7 @@
     if not fits_kernel(sizes, rows, cols, chans, hidden, residues):
         return local(pair_map, residue_mask, proj_weight, gate_weight, out_weight)
     groups = sizes["gy"] * sizes["gz"]
-    main = rows // HALF_LANES * HALF_LANES
+    main = main_rows(rows)
     dma = pltpu.SemaphoreType.DMA
     vmem = pl.BlockSpec(memory_space=pltpu.VMEM)
     turned = pl.pallas_call(

time: 26.3 us -> 25.3 us (0.962)
  Pallas kernels: 25.5 us -> 24.4 us
    pallas_call x1, Pallas kernels: 25.5 us -> 24.4 us  [local_fused(): pl.pallas_call(functools.partial(fused_kernel, sizes['gy'], sizes['gz'],...]
where the time goes in v3:
time: 25.3 us; the launch traced here: 25.1 us
  Pallas kernels  24.4 us (96%)
  local copies, waits for them, and re-layouts  0.68 us (3%)
    pallas_call x1, Pallas kernels, local_fused(): pl.pallas_call(functools.partial(fused_kernel, sizes['gy'], sizes['gz'],...  24.4 us
    unnamed x1, local copies, waits for them, and re-layouts  0.68 us

profile of v3, /device:TPU:0, one launch (start us, length us, event | category | flops | bytes accessed | tf_op | source)
XLA Modules:
  0.0 25.1 jit_solution(4447710255088843766)
XLA Ops:
  0.0 24.4 %shard_map.55 = bf16[10,80,128]{2,1,0:T(8,128)(2,1)S(1)} custom-call(bf16[10,80,128]{2,1,0:T(8,128)(2,1)} %bitcast.4, s32[1,160]{1,0:T(1,128)} %bitcast.5, bf16[128,512]{1,0:T(8,128)(2,1)} %proj_hbm.1, bf16[128,128]{1,0:T(8,128)(2,1)} %gate_hbm.1, bf16[128,128]{1,0:T(8,128)(2,1)} %out_w_hbm.1), custom_call_target="tpu_custom_call" | custom-call | tf_op jit(solution)/shard_map/pallas_call | solution.py:622
  24.4 0.7 %copy.7 = bf16[80,10,128]{2,0,1:T(8,128)(2,1)} copy(bf16[80,10,128]{2,0,1:T(8,128)(2,1)S(1)} %bitcast.3) | data formatting | bytes 409600

commit v4 on v3

--- a/solution.py
+++ b/solution.py
@@ -138,6 +138,10 @@
     return -(-value // step) * step
 
 
+def folded(count):
+    return count // LANES * LANES * 2 + LANES
+
+
 def main_rows(rows):
     return rows * 8 // 10 // 16 * 16
 
@@ -150,7 +154,7 @@
     along_y, along_z, main,
     pair_hbm, mask_hbm, proj_hbm, gate_hbm, out_w_hbm, out_ref,
     pair_ref, mask_ref, proj_ref, gate_ref, out_w_ref,
-    proj_s, normed_bf, masked_bf, gate_f32, send_r, recv_r, recv_x, send_l, recv_l,
+    proj_s, normed_bf, masked_bf, gate_f32, send_r, recv_r, recv_x, send_s, recv_s, send_l, recv_l,
     left_s, edge_s, edge_bf, right_s, right_bf, tri_s, send_e, recv_e, send_b, recv_b,
     load_sem, send_sem, rsem_r, rsem_x, rsem_l, rsem_b,
 ):
@@ -161,8 +165,6 @@
     edge = rows - main
     flat_m, flat_e = main * cols, edge * cols
     flat = flat_m + flat_e
-    wide = up(flat, LANES)
-    both = up(flat + flat_e, LANES)
     residues = mask_ref.shape[1]
     px, py, pz = lax.axis_index("gx"), lax.axis_index("gy"), lax.axis_index("gz")
     me = py * along_z + pz
@@ -224,6 +226,28 @@
                 target[k * main : (k + 1) * main, :] = value[0:main]
                 target[flat_m + k * edge : flat_m + (k + 1) * edge, :] = value[main:rows]
 
+    lane8 = lax.broadcasted_iota(jnp.int32, (gc, LANES), 1)
+    hg = gc // 2
+
+    def fold(value):
+        count = value.shape[1]
+        body, rest = count // LANES * LANES, count % LANES
+        value = jnp.concatenate([value, jnp.zeros((gc, LANES - rest), jnp.float32)], axis=1)
+        lower = pltpu.roll(value, hg, 0)
+        tail = jnp.where(lane8 < rest, value[:, body:], pltpu.roll(lower[:, body:], rest, 1))
+        return jnp.concatenate([value[:, 0:body], lower[:, 0:body], tail], axis=1)[
+            0:hg
+        ].astype(jnp.bfloat16)
+
+    def unfold(value, count):
+        body, rest = count // LANES * LANES, count % LANES
+        tail = value[:, 2 * body : 2 * body + LANES]
+        upper = jnp.concatenate([value[:, 0:body], tail], axis=1)
+        lower = jnp.concatenate(
+            [value[:, body : 2 * body], pltpu.roll(tail, LANES - rest, 1)], axis=1
+        )
+        return jnp.concatenate([upper, lower], axis=0)
+
     half = hidden // 2
     half_groups = groups // 2
 
@@ -243,22 +267,20 @@
 
     def copy_r(d, slot):
         return pltpu.make_async_remote_copy(
-            src_ref=send_r.at[d, :, 0:wide], dst_ref=recv_r.at[slot, :, 0:wide],
-            send_sem=send_sem.at[0], recv_sem=rsem_r.at[slot], device_id=place(d),
-            device_id_type=MESH,
-        )
-
-    def copy_rest(d, slot, n, count=1):
+            src_ref=send_r.at[d], dst_ref=recv_r.at[slot], send_sem=send_sem.at[0],
+            recv_sem=rsem_r.at[slot], device_id=place(d), device_id_type=MESH,
+        )
+
+    def copy_rest(d, slot, count=1):
         return pltpu.make_async_remote_copy(
-            src_ref=send_r.at[pl.ds(d, count), :, wide:both],
-            dst_ref=recv_r.at[pl.ds(slot, count), :, wide:both],
-            send_sem=send_sem.at[5], recv_sem=rsem_l.at[n + along_z], device_id=place(d),
+            src_ref=send_s.at[pl.ds(d, count)], dst_ref=recv_s.at[pl.ds(slot, count)],
+            send_sem=send_sem.at[5], recv_sem=rsem_b.at[2], device_id=place(d),
             device_id_type=MESH,
         )
 
     def copy_x(s, n, count=1):
         return pltpu.make_async_remote_copy(
-            src_ref=recv_r.at[pl.ds(s, count), :, 0:wide], dst_ref=recv_x.at[pl.ds(s, count)],
+            src_ref=recv_r.at[pl.ds(s, count)], dst_ref=recv_x.at[pl.ds(s, count)],
             send_sem=send_sem.at[1], recv_sem=rsem_x.at[n],
             device_id=partner, device_id_type=MESH,
         )
@@ -284,11 +306,10 @@
         with jax.named_scope(f"gated_r{turn}"):
             value = gated(2 * hidden, first, 0, flat)
             extra = gated(0, first, flat_m, flat)
-            value = jnp.concatenate([value, extra], axis=1)
             for part in range(half_groups):
-                send_r[first // gc + part, :, 0 : flat + flat_e] = value[
-                    part * gc : (part + 1) * gc
-                ].astype(jnp.bfloat16)
+                at = slice(part * gc, (part + 1) * gc)
+                send_r[first // gc + part] = fold(value[at])
+                send_s[first // gc + part] = fold(extra[at])
         if turn == 0:
             with jax.named_scope("barrier"):
                 pl.semaphore_wait(barrier, groups)
@@ -306,8 +327,10 @@
                     for plane in (far_a, far_b, sibling, py):
                         if n == 0 and plane is py:
                             continue
-                        copy_rest(to(plane, n), me, n).start()
+                        copy_rest(to(plane, n), me).start()
     recv_r[me] = send_r[me]
+    recv_s[me] = send_s[me]
+    copy_x(me, 0).start()
 
     for turn in range(2):
         first = (1 - side if turn == 0 else side) * half
@@ -326,8 +349,6 @@
             0.5 * jnp.dot(normed_bf[...], gate_ref[...], preferred_element_type=jnp.float32)
         )
 
-    lane8 = lax.broadcasted_iota(jnp.int32, (gc, LANES), 1)
-
     def lift(value, begin, width, lane):
         low, high = begin // LANES, (begin + width - 1) // LANES
         shift = (lane - begin) % LANES
@@ -362,8 +383,7 @@
         copy_x(s, n).start()
 
     def spread_r(s):
-        value = recv_r[s, :, 0:wide].astype(jnp.float32)
-        spread_right(value, s, right_s.at[px])
+        spread_right(unfold(recv_r[s].astype(jnp.float32), flat), s, right_s.at[px])
 
     def take_plane(plane, first):
         for n in range(first, along_z):
@@ -388,7 +408,6 @@
 
         return carry
 
-    copy_x(me, 0).start()
     with jax.named_scope("take_own"):
         take_plane(py, 1)
     with jax.named_scope("take_far0"):
@@ -399,8 +418,7 @@
         take_far(1, 0)
     with jax.named_scope("wait_send"):
         pltpu.make_async_remote_copy(
-            src_ref=send_r.at[0 : groups - 1, :, 0:wide],
-            dst_ref=recv_r.at[0 : groups - 1, :, 0:wide],
+            src_ref=send_r.at[0 : groups - 1], dst_ref=recv_r.at[0 : groups - 1],
             send_sem=send_sem.at[0], recv_sem=rsem_r.at[0], device_id=partner,
             device_id_type=MESH,
         ).wait_send()
@@ -411,38 +429,27 @@
     with jax.named_scope("take_far3"):
         take_far(3, 0)
 
-    rest_low = flat // LANES * LANES
+    copy_rest(0, 0, groups - 1).wait_recv()
 
     def take_rest(n, carry):
-        @pl.when(n == 0)
-        def _():
-            copy_rest(0, 0, 0, along_y - 1).wait_recv()
-
-        @pl.when(n > 0)
-        def _():
-            copy_rest(0, 0, n, along_y).wait_recv()
-
         for plane in planes:
             s = to(plane, n)
-            value = recv_r[s, :, rest_low:both].astype(jnp.float32)
+            value = unfold(recv_s[s].astype(jnp.float32), flat_e)
             for k in range(cols):
                 at = pl.multiple_of((s * cols + k) * gc, gc)
-                edge_s[pl.ds(at, gc), :] = lift(value, flat + k * edge - rest_low, edge, 0)
+                edge_s[pl.ds(at, gc), :] = lift(value, k * edge, edge, 0)
         return carry
 
     with jax.named_scope("take_rest"):
-        lax.fori_loop(0, along_z, take_rest, 0)
+        lax.fori_loop(0, along_z, take_rest, 0, unroll=True)
 
     def tri(left, width, c, h, first):
         if first:
-            right = right_s[h, pl.ds(c, residues, stride=gc), :].astype(jnp.bfloat16)
+            right = right_s[h, pl.ds(c, residues, stride=gc), :].T.astype(jnp.bfloat16)
             right_bf[h, c] = right
         else:
             right = right_bf[h, c]
-        block = lax.dot_general(
-            right[:, 0:rows], left[:, 0:width], (((0,), (0,)), ((), ())),
-            preferred_element_type=jnp.float32,
-        )
+        block = jnp.dot(right[0:rows], left[:, 0:width], preferred_element_type=jnp.float32)
         at = pl.multiple_of(h * rows * gc, gc)
         tri_s[pl.ds(at + c, rows, stride=gc), 0:width] = block
 
@@ -454,13 +461,13 @@
 
     def take_x(n, carry):
         pltpu.make_async_remote_copy(
-            src_ref=recv_r.at[0:along_y, :, 0:wide], dst_ref=recv_x.at[0:along_y],
+            src_ref=recv_r.at[0:along_y], dst_ref=recv_x.at[0:along_y],
             send_sem=send_sem.at[1], recv_sem=rsem_x.at[n], device_id=partner,
             device_id_type=MESH,
         ).wait_recv()
         for plane in planes:
             s = to(plane, n)
-            spread_right(recv_x[s].astype(jnp.float32), s, right_s.at[1 - px])
+            spread_right(unfold(recv_x[s].astype(jnp.float32), flat), s, right_s.at[1 - px])
         return carry
 
     with jax.named_scope("take_x"):
@@ -477,23 +484,30 @@
             blocks[n] = piece if shift == 0 else jnp.where(lane8 < shift, blocks[n], piece)
             if shift + width > LANES:
                 blocks[n + 1] = piece
-        return jnp.concatenate(blocks, axis=1).astype(jnp.bfloat16)
+        value = jnp.concatenate(blocks, axis=1)
+        if width == main:
+            return value.astype(jnp.bfloat16)
+        return fold(value[:, 0 : cols * width])
 
     def ship(width, buffer, landed, copy):
-        def around(n, carry):
-            goals = [to(plane, n) for plane in (far_a, far_b, sibling, py)]
+        def fill(goals):
             packed = [pack(d, width) for d in goals]
             for d, value in zip(goals, packed):
                 buffer[d] = value
+
+        def begin(goals):
             for d in goals:
 
                 @pl.when(d != me)
                 def _():
                     copy(d, me).start()
 
-            return carry
-
-        lax.fori_loop(0, along_z, around, 0)
+        far = [to(plane, n) for n in range(along_z) for plane in (far_a, far_b)]
+        near = [to(plane, n) for n in range(along_z) for plane in (sibling, py)]
+        fill(far)
+        begin(far)
+        fill(near)
+        begin(near)
         landed[me] = buffer[me]
 
     with jax.named_scope("tri_e"):
@@ -502,22 +516,13 @@
     with jax.named_scope("ship_e"):
         ship(edge, send_e, recv_e, copy_e)
 
-    def take_l(n, carry):
-        @pl.when(n == 0)
-        def _():
-            copy_l(0, 0, 0, along_y - 1).wait_recv()
-
-        @pl.when(n > 0)
-        def _():
-            copy_l(0, 0, n, along_y).wait_recv()
-
-        for plane in planes:
-            s = to(plane, n)
-            spread_main(recv_l[s].astype(jnp.float32), s, left_s)
-        return carry
-
     with jax.named_scope("take_l"):
-        lax.fori_loop(0, along_z, take_l, 0)
+        for n in range(along_z):
+            copy_l(0, 0, n, along_y if n else along_y - 1).wait_recv()
+        for n in range(along_z):
+            for plane in planes:
+                s = to(plane, n)
+                spread_main(recv_l[s].astype(jnp.float32), s, left_s)
     with jax.named_scope("tri_m"):
         for c in range(gc):
             left = left_s[pl.ds(c, residues, stride=gc), :].astype(jnp.bfloat16)
@@ -528,7 +533,14 @@
 
     def final(received, low, width):
         count = width * cols
-        triangle = received[:, :, 0:count].astype(jnp.float32).reshape(hidden, count)
+        if width == main:
+            triangle = received[:, :, 0:count].astype(jnp.float32)
+        else:
+            triangle = jnp.concatenate(
+                [unfold(received[s].astype(jnp.float32), count)[:, 0:count] for s in range(groups)],
+                axis=0,
+            )
+        triangle = triangle.reshape(hidden, count)
         normed_tri = layer_norm_lead(triangle).astype(jnp.bfloat16)
         mixed = lax.dot_general(
             normed_tri, out_w_ref[...], (((0,), (0,)), ((), ())),
@@ -544,7 +556,7 @@
     with jax.named_scope("final_e"):
         final(recv_e, main, edge)
     with jax.named_scope("finish"):
-        copy_rest(0, 0, 0, groups - 1).wait_send()
+        copy_rest(0, 0, groups - 1).wait_send()
         copy_x(0, 0, groups).wait_send()
         copy_l(0, 0, 0, groups - 1).wait_send()
         copy_e(0, 0, groups - 1).wait_send()
@@ -559,8 +571,7 @@
 def scratch_list(main, rows, cols, chans, hidden, groups, residues):
     gc = hidden // groups
     flat_m, flat_e = main * cols, (rows - main) * cols
-    wide = up(flat_m + flat_e, LANES)
-    both = up(flat_m + 2 * flat_e, LANES)
+    flat = flat_m + flat_e
     bf, f32 = jnp.bfloat16, jnp.float32
     return [
         ((cols, rows, chans), bf),
@@ -572,19 +583,21 @@
         ((rows * cols, chans), bf),
         ((rows * cols, chans), bf),
         ((rows * cols, chans), f32),
-        ((groups, gc, both), bf),
-        ((groups, gc, both), bf),
-        ((groups, gc, wide), bf),
+        ((groups, gc // 2, folded(flat)), bf),
+        ((groups, gc // 2, folded(flat)), bf),
+        ((groups, gc // 2, folded(flat)), bf),
+        ((groups, gc // 2, folded(flat_e)), bf),
+        ((groups, gc // 2, folded(flat_e)), bf),
         ((groups, gc, up(flat_m, LANES)), bf),
         ((groups, gc, up(flat_m, LANES)), bf),
         ((residues * gc, LANES), f32),
         ((residues * gc, LANES), f32),
         ((gc, residues, LANES), bf),
         ((2, residues * gc, LANES), f32),
-        ((2, gc, residues, LANES), bf),
+        ((2, gc, LANES, residues), bf),
         ((residues * gc, LANES), f32),
-        ((groups, gc, up(flat_e, LANES)), bf),
-        ((groups, gc, up(flat_e, LANES)), bf),
+        ((groups, gc // 2, folded(flat_e)), bf),
+        ((groups, gc // 2, folded(flat_e)), bf),
         ((groups, gc, up(flat_m, LANES)), bf),
         ((groups, gc, up(flat_m, LANES)), bf),
     ]
@@ -599,6 +612,8 @@
     if sizes["gy"] != 4 or sizes["gz"] != 4 or residues != 2 * rows or residues != groups * cols:
         return False
     if chans != LANES or rows > LANES or rows % 16 or main < 16 or edge < 16:
+        return False
+    if rows * cols % LANES * 2 > LANES or edge * cols % LANES * 2 > LANES:
         return False
     total = 0
     for shape, kind in scratch_list(main, rows, cols, chans, hidden, groups, residues):
@@ -628,7 +643,7 @@
             pltpu.VMEM(shape, kind)
             for shape, kind in scratch_list(main, rows, cols, chans, hidden, groups, residues)
         ]
-        + [dma((5,)), dma((6,)), dma((groups,)), dma((sizes["gz"],)), dma((2 * sizes["gz"],)), dma((2,))],
+        + [dma((5,)), dma((6,)), dma((groups,)), dma((sizes["gz"],)), dma((sizes["gz"],)), dma((3,))],
         compiler_params=pltpu.CompilerParams(
             collective_id=0, has_side_effects=True, vmem_limit_bytes=VMEM_ALL - 204800
         ),

time: 25.3 us -> 24.9 us (0.984)
  Pallas kernels: 24.4 us -> 24 us
    pallas_call x1, Pallas kernels: 24.4 us -> 24 us  [local_fused(): pl.pallas_call(functools.partial(fused_kernel, sizes['gy'], sizes['gz'],...]
where the time goes in v4:
time: 24.9 us; the launch traced here: 24.7 us
  Pallas kernels  24 us (96%)
  local copies, waits for them, and re-layouts  0.68 us (3%)
    pallas_call x1, Pallas kernels, local_fused(): pl.pallas_call(functools.partial(fused_kernel, sizes['gy'], sizes['gz'],...  24 us
    unnamed x1, local copies, waits for them, and re-layouts  0.68 us

profile of v4, /device:TPU:0, one launch (start us, length us, event | category | flops | bytes accessed | tf_op | source)
XLA Modules:
  0.0 24.7 jit_solution(2545898225764407430)
XLA Ops:
  0.0 24.0 %shard_map.55 = bf16[10,80,128]{2,1,0:T(8,128)(2,1)S(1)} custom-call(bf16[10,80,128]{2,1,0:T(8,128)(2,1)} %bitcast.4, s32[1,160]{1,0:T(1,128)} %bitcast.5, bf16[128,512]{1,0:T(8,128)(2,1)} %proj_hbm.1, bf16[128,128]{1,0:T(8,128)(2,1)} %gate_hbm.1, bf16[128,128]{1,0:T(8,128)(2,1)} %out_w_hbm.1), custom_call_target="tpu_custom_call" | custom-call | tf_op jit(solution)/shard_map/pallas_call | solution.py:637
  24.0 0.7 %copy.7 = bf16[80,10,128]{2,0,1:T(8,128)(2,1)} copy(bf16[80,10,128]{2,0,1:T(8,128)(2,1)S(1)} %bitcast.3) | data formatting | bytes 409600

commit v5 on v4

--- a/solution.py
+++ b/solution.py
@@ -317,8 +317,8 @@
             if turn == 0:
                 order = [(plane, n) for n in range(2) for plane in (far_a, far_b)]
             else:
-                order = [(py, n) for n in range(1, along_z)]
-                order += [(sibling, n) for n in range(along_z)]
+                order = [(sibling, n) for n in range(along_z)]
+                order += [(py, n) for n in range(1, along_z)]
                 order += [(plane, n) for n in range(2, along_z) for plane in (far_a, far_b)]
             for plane, n in order:
                 copy_r(to(plane, n), me).start()
@@ -398,15 +398,10 @@
             spread_r(to(plane, n))
         return carry
 
-    def start_l(n, carry):
+    def start_l():
         for plane in (far_a, far_b, sibling, py):
-            d = to(plane, n)
-
-            @pl.when(d != me)
-            def _():
-                copy_l(d, me, n).start()
-
-        return carry
+            for n in range(0 if plane is not py else 1, along_z):
+                copy_l(to(plane, n), me, n).start()
 
     with jax.named_scope("take_own"):
         take_plane(py, 1)
@@ -423,7 +418,7 @@
             device_id_type=MESH,
         ).wait_send()
     with jax.named_scope("start_l"):
-        lax.fori_loop(0, along_z, start_l, 0)
+        start_l()
     with jax.named_scope("take_far2"):
         take_far(2, 0)
     with jax.named_scope("take_far3"):
@@ -502,7 +497,7 @@
                 def _():
                     copy(d, me).start()
 
-        far = [to(plane, n) for n in range(along_z) for plane in (far_a, far_b)]
+        far = [to(plane, n) for plane in (far_a, far_b) for n in range(along_z)]
         near = [to(plane, n) for n in range(along_z) for plane in (sibling, py)]
         fill(far)
         begin(far)

time: 24.9 us -> 24.4 us (0.980)
  Pallas kernels: 24 us -> 23.6 us
    pallas_call x1, Pallas kernels: 24 us -> 23.6 us  [local_fused(): pl.pallas_call(functools.partial(fused_kernel, sizes['gy'], sizes['gz'],...]
where the time goes in v5:
time: 24.4 us; the launch traced here: 24.3 us
  Pallas kernels  23.6 us (97%)
  local copies, waits for them, and re-layouts  0.68 us (3%)
    pallas_call x1, Pallas kernels, local_fused(): pl.pallas_call(functools.partial(fused_kernel, sizes['gy'], sizes['gz'],...  23.6 us
    unnamed x1, local copies, waits for them, and re-layouts  0.68 us

profile of v5, /device:TPU:0, one launch (start us, length us, event | category | flops | bytes accessed | tf_op | source)
XLA Modules:
  0.0 24.3 jit_solution(7112065592652203159)
XLA Ops:
  0.0 23.6 %shard_map.55 = bf16[10,80,128]{2,1,0:T(8,128)(2,1)S(1)} custom-call(bf16[10,80,128]{2,1,0:T(8,128)(2,1)} %bitcast.4, s32[1,160]{1,0:T(1,128)} %bitcast.5, bf16[128,512]{1,0:T(8,128)(2,1)} %proj_hbm.1, bf16[128,128]{1,0:T(8,128)(2,1)} %gate_hbm.1, bf16[128,128]{1,0:T(8,128)(2,1)} %out_w_hbm.1), custom_call_target="tpu_custom_call" | custom-call | tf_op jit(solution)/shard_map/pallas_call | solution.py:632
  23.6 0.7 %copy.7 = bf16[80,10,128]{2,0,1:T(8,128)(2,1)} copy(bf16[80,10,128]{2,0,1:T(8,128)(2,1)S(1)} %bitcast.3) | data formatting | bytes 409600

commit v6 on v5

--- a/solution.py
+++ b/solution.py
@@ -293,7 +293,7 @@
         )
 
     def copy_l(d, slot, n, count=1):
-        return copy_many(send_l, recv_l, 2, rsem_l.at[n], d, slot, count)
+        return copy_many(send_l, recv_l, 2, rsem_l.at[0], d, slot, count)
 
     def copy_e(d, slot, count=1):
         return copy_many(send_e, recv_e, 3, rsem_b.at[0], d, slot, count)
@@ -498,7 +498,7 @@
                     copy(d, me).start()
 
         far = [to(plane, n) for plane in (far_a, far_b) for n in range(along_z)]
-        near = [to(plane, n) for n in range(along_z) for plane in (sibling, py)]
+        near = [to(plane, n) for plane in (sibling, py) for n in range(along_z)]
         fill(far)
         begin(far)
         fill(near)
@@ -512,8 +512,7 @@
         ship(edge, send_e, recv_e, copy_e)
 
     with jax.named_scope("take_l"):
-        for n in range(along_z):
-            copy_l(0, 0, n, along_y if n else along_y - 1).wait_recv()
+        copy_l(0, 0, 0, groups - 1).wait_recv()
         for n in range(along_z):
             for plane in planes:
                 s = to(plane, n)
@@ -638,7 +637,7 @@
             pltpu.VMEM(shape, kind)
             for shape, kind in scratch_list(main, rows, cols, chans, hidden, groups, residues)
         ]
-        + [dma((5,)), dma((6,)), dma((groups,)), dma((sizes["gz"],)), dma((sizes["gz"],)), dma((3,))],
+        + [dma((5,)), dma((6,)), dma((groups,)), dma((sizes["gz"],)), dma((1,)), dma((3,))],
         compiler_params=pltpu.CompilerParams(
             collective_id=0, has_side_effects=True, vmem_limit_bytes=VMEM_ALL - 204800
         ),

time: 24.4 us -> 24.4 us (level)
  no operation moved by 1% of the time
where the time goes in v6:
time: 24.4 us; the launch traced here: 24.2 us
  Pallas kernels  23.5 us (96%)
  local copies, waits for them, and re-layouts  0.68 us (3%)
    pallas_call x1, Pallas kernels, local_fused(): pl.pallas_call(functools.partial(fused_kernel, sizes['gy'], sizes['gz'],...  23.5 us
    unnamed x1, local copies, waits for them, and re-layouts  0.68 us

profile of v6, /device:TPU:0, one launch (start us, length us, event | category | flops | bytes accessed | tf_op | source)
XLA Modules:
  0.0 24.2 jit_solution(15038982995348296478)
XLA Ops:
  0.0 23.5 %shard_map.55 = bf16[10,80,128]{2,1,0:T(8,128)(2,1)S(1)} custom-call(bf16[10,80,128]{2,1,0:T(8,128)(2,1)} %bitcast.4, s32[1,160]{1,0:T(1,128)} %bitcast.5, bf16[128,512]{1,0:T(8,128)(2,1)} %proj_hbm.1, bf16[128,128]{1,0:T(8,128)(2,1)} %gate_hbm.1, bf16[128,128]{1,0:T(8,128)(2,1)} %out_w_hbm.1), custom_call_target="tpu_custom_call" | custom-call | tf_op jit(solution)/shard_map/pallas_call | solution.py:631
  23.6 0.7 %copy.7 = bf16[80,10,128]{2,0,1:T(8,128)(2,1)} copy(bf16[80,10,128]{2,0,1:T(8,128)(2,1)S(1)} %bitcast.3) | data formatting | bytes 409600
